TPU v7x, 32 devices: a whole 2x2x4 slice. The times are simulated.
32 devices in a mesh: group: 2 (over y), batch: 4 (over z), expert: 4 (over x, core).
Axes of the slice: x: 2, y: 2, z: 4, core: 2. Of those that a mesh axis runs over, the one named last changes fastest.
Arguments:
- residual_in: bfloat16 [128, 4096], P(('group', 'batch')), parts along dimension 0, may hold values from -11 to 11
- queries: bfloat16 [128, 16, 128], P(('group', 'batch'), 'expert'), parts along dimension 0, may hold values from -150 to 150
- key_new: bfloat16 [128, 4, 128], P(('group', 'batch'), 'expert'), parts along dimension 0, may hold values from -6 to 6
- value_new: bfloat16 [128, 4, 128], P(('group', 'batch'), 'expert'), parts along dimension 0, may hold values from -6 to 6
- key_cache: bfloat16 [128, 4, 256, 128], P(('group', 'batch'), 'expert'), parts along dimension 0, may hold values from -6 to 6
- value_cache: bfloat16 [128, 4, 256, 128], P(('group', 'batch'), 'expert'), parts along dimension 0, may hold values from -6 to 6
- cache_len: int32 [128], P(('group', 'batch')), parts along dimension 0, may hold values from 1 to 256, 8192 in all
- new_slot: int32 [128], P(('group', 'batch')), parts along dimension 0, may hold values 0 or 1
- out_weight: bfloat16 [2048, 4096], P('expert'), may hold values from -0.125 to 0.125
- norm_gain: float32 [4096], replicated, may hold values from 0.5 to 1.5
- router: bfloat16 [4096, 4], replicated, may hold values from -0.09375 to 0.09375
- chosen: int32 [128, 2], P(('group', 'batch')), parts along dimension 0, may hold values from 0 to 3, all different within a row; in each aligned block of 16 rows (0 to 15, 16 to 31, ...) at most 12 rows name the same one
- w_gate: bfloat16 [4, 4096, 8192], P('expert', None, 'batch'), may hold values from -0.09375 to 0.09375
- w_up: bfloat16 [4, 4096, 8192], P('expert', None, 'batch'), may hold values from -0.09375 to 0.09375
- w_down: bfloat16 [4, 8192, 4096], P('expert', 'batch'), may hold values from -0.0625 to 0.0625
Outputs:
- layer_out: bfloat16 [128, 4096], P(('group', 'batch', 'expert')), parts along dimension 0
There are 2 independent parts, one for each index of `group`. A program takes and returns all parts, laid end to end along the dimension named above; an argument that names none is the same for every part. Nothing has to cross between parts.
Inputs may be any that keep to these rules, and one draw needn't show every extreme that they name: `chosen`: each row names 2 different experts. Among the rows of one device no expert is named by more than 12 rows, and in every draw some expert is named by exactly 12 rows of some device. `cache_len`: the lengths of a part sum to 8192, and the largest is exactly 256.
All inputs are finite; a program needn't handle non-finite values. No bound on the sum of `cache_len` or of `new_slot` on one device may be relied on, other than what follows from the above.
Results may differ from a plain program's by a relative error of at most 0.017.
Values may be sent and summed in bfloat16 or wider, within the bound.
No kernel may reach another device: no remote copies, remote signals or barrier semaphores. Data moves between devices by JAX's collectives and lax.ppermute only.
A program may use at most 128 MiB of HBM per device.

v0:
```python
import jax
import jax.numpy as jnp
from jax import lax
from jax.sharding import PartitionSpec as P

CAP = 12
epsilon = 1e-05


def attend(queries, key_new, value_new, key_cache, value_cache, cache_len, new_slot):
    slot_count, kv_count, length, head_width = key_cache.shape
    group_size = queries.shape[1] // kv_count
    grouped = queries.reshape(slot_count, kv_count, group_size, head_width)
    scaling = float(head_width) ** (-0.5)
    scores = (
        jnp.einsum("skgd,sktd->skgt", grouped, key_cache, preferred_element_type=jnp.float32)
        * scaling
    )
    own_score = (
        jnp.einsum("skgd,skd->skg", grouped, key_new, preferred_element_type=jnp.float32) * scaling
    )
    places = lax.broadcasted_iota(jnp.int32, (slot_count, length), 1)
    usable = (places < cache_len[:, None]) & (new_slot[:, None] == 0)
    usable = usable[:, None, None, :]
    scores = jnp.where(usable, scores, jnp.float32(-1e30))
    highest = jnp.maximum(jnp.max(scores, axis=3), own_score)
    weights = jnp.where(usable, jnp.exp(scores - highest[..., None]), jnp.float32(0.0))
    own_weight = jnp.exp(own_score - highest)
    denominator = jnp.sum(weights, axis=3) + own_weight
    probabilities = (weights / denominator[..., None]).astype(jnp.bfloat16)
    own_prob = (own_weight / denominator).astype(jnp.bfloat16)
    attended = jnp.einsum(
        "skgt,sktd->skgd", probabilities, value_cache, preferred_element_type=jnp.float32
    )
    attended = (
        attended
        + own_prob.astype(jnp.float32)[..., None] * value_new.astype(jnp.float32)[:, :, None, :]
    )
    return attended.reshape(slot_count, kv_count * group_size * head_width).astype(jnp.bfloat16)


def mixing(logits, chosen, expert_count):
    labels = lax.broadcasted_iota(jnp.int32, (1, 1, expert_count), 2)
    picking = (chosen[:, :, None] == labels).astype(jnp.float32)
    chosen_logits = jnp.sum(picking * logits[:, None, :], axis=2)
    leading = jax.nn.sigmoid(chosen_logits[:, 0] - chosen_logits[:, 1])
    fractions = jnp.stack([leading, 1.0 - leading], axis=1)
    return jnp.sum(picking * fractions[:, :, None], axis=1)


def placement_table(chosen, targets, capacity):
    routed = jnp.sum((chosen[None, :, :] == targets[:, None, None]).astype(jnp.int32), axis=2)
    position = jnp.cumsum(routed, axis=1) - routed
    row_labels = lax.broadcasted_iota(jnp.int32, (1, capacity, 1), 1)
    return ((position[:, None, :] == row_labels) & (routed[:, None, :] == 1)).astype(jnp.float32)


def body(
    residual_in,
    queries,
    key_new,
    value_new,
    key_cache,
    value_cache,
    cache_len,
    new_slot,
    out_weight,
    norm_gain,
    router,
    chosen,
    w_gate,
    w_up,
    w_down,
):
    my_expert = lax.axis_index("expert")
    attended = attend(queries, key_new, value_new, key_cache, value_cache, cache_len, new_slot)
    partial_value = jnp.dot(attended, out_weight, preferred_element_type=jnp.float32)
    summed = lax.psum(partial_value, "expert")
    stream = (residual_in.astype(jnp.float32) + summed).astype(jnp.bfloat16)
    values = stream.astype(jnp.float32)
    scaling = lax.rsqrt(jnp.mean(values * values, axis=1, keepdims=True) + epsilon)
    normed = (values * scaling * norm_gain).astype(jnp.bfloat16)
    logits = jnp.dot(normed, router, preferred_element_type=jnp.float32)
    placing = placement_table(chosen, jnp.reshape(my_expert, (1,)), CAP)[0]
    sent_rows = jnp.dot(
        placing.astype(jnp.bfloat16), normed, preferred_element_type=jnp.float32
    ).astype(jnp.bfloat16)
    carried = values * (my_expert == 0).astype(jnp.float32)
    coef = mixing(logits, chosen, router.shape[1])
    expert_labels = lax.broadcasted_iota(jnp.int32, (1, router.shape[1]), 1)
    my_coef = jnp.sum(coef * (expert_labels == my_expert).astype(jnp.float32), axis=1)
    row_weight = jnp.dot(placing, my_coef, precision=lax.Precision.HIGHEST)
    block_rows = lax.all_gather(sent_rows, "batch", axis=0, tiled=True)
    gate_part = jnp.dot(block_rows, w_gate[0], preferred_element_type=jnp.float32)
    up_part = jnp.dot(block_rows, w_up[0], preferred_element_type=jnp.float32)
    hidden = (jax.nn.silu(gate_part) * up_part).astype(jnp.bfloat16)
    block_rows = hidden
    outputs = lax.psum_scatter(
        jnp.dot(block_rows, w_down[0], preferred_element_type=jnp.float32).astype(jnp.bfloat16),
        "batch",
        scatter_dimension=0,
        tiled=True,
    ).astype(jnp.float32)
    weighted = row_weight[:, None] * outputs
    contribution = jnp.dot(placing.T, weighted, precision=lax.Precision.HIGHEST) + carried
    layer_out = lax.psum_scatter(
        contribution.astype(jnp.bfloat16), "expert", scatter_dimension=0, tiled=True
    )
    return layer_out


def solution(mesh):
    in_specs = (
        P(("group", "batch"), None),
        P(("group", "batch"), "expert", None),
        P(("group", "batch"), "expert", None),
        P(("group", "batch"), "expert", None),
        P(("group", "batch"), "expert", None, None),
        P(("group", "batch"), "expert", None, None),
        P(("group", "batch")),
        P(("group", "batch")),
        P("expert", None),
        P(),
        P(),
        P(("group", "batch"), None),
        P("expert", None, "batch"),
        P("expert", None, "batch"),
        P("expert", "batch", None),
    )
    out_specs = P(("group", "batch", "expert"), None)
    return jax.shard_map(body, mesh=mesh, in_specs=in_specs, out_specs=out_specs, check_vma=False)
```

profile of v0, /device:TPU:0, one launch (start us, length us, event | category | flops | bytes accessed | tf_op | source)
XLA Modules:
  0.0 154.4 jit_solution(7242869067965577408)
XLA Ops:
  6.5 0.0 copy-start
  6.5 0.0 all-reduce.6.cloned.1.call-start
  6.5 0.7 broadcast_compare_fusion
  7.3 0.7 fusion.48
  8.0 0.9 fusion.52
  8.9 0.0 copy-done
  8.9 1.2 fusion.67
  10.1 0.2 fusion.37
  10.3 0.7 bitcast_convert_fusion
  11.0 1.5 fusion.19
  12.5 3.6 %fusion.45 = f32[16,4096]{1,0:T(8,128)} fusion(bf16[512,4096]{1,0:T(8,128)(2,1)} %param.23, bf16[2,8,4,128]{3,2,1,0:T(4,128)(2,1)S(1)} %bitcast.56), kind=kOutput, calls=%fused_computation.45 | convolution fusion | flops 67108864 | bytes 4472832 | tf_op jit(solution)/shard_map/dot_general | solution.py:77
  16.1 0.0 all-reduce.6.cloned.1.call-update
  16.1 0.0 all-reduce.8.cloned.1.call-start
  16.1 0.7 fusion.63
  16.8 0.1 copy.26
  17.0 0.1 reduce.6
  17.1 1.2 dynamic-slice.6
  19.0 32.2 %all-reduce.6.cloned.1.call-done = f32[16,4096]{1,0:T(8,128)} async-done(((f32[16,4096]{1,0:T(8,128)}), f32[16,4096]{1,0:T(8,128)}) %all-reduce.6.cloned.1.call-update) | async-done | bytes 262160 | tf_op jit(solution)/shard_map/psum | solution.py:78
  51.2 1.1 fusion.29
  52.4 1.0 fusion.11
  53.3 15.2 %all-gather = bf16[4,12,4096]{2,1,0:T(8,128)(2,1)S(1)} all-gather(bf16[1,12,4096]{2,1,0:T(8,128)(2,1)S(1)} %fusion.11), channel_id=1, replica_groups=mesh['group'=2,'batch'=4,'expert'=4] {'batch'}, dimensions={0}, use_global_device_ids=true | all-gather | bytes 491520 | tf_op jit(solution)/shard_map/all_gather | solution.py:93
  68.5 0.1 reshape.221
  68.6 8.8 %fusion.5 = f32[48,2048]{1,0:T(8,128)S(1)} fusion(bf16[48,4096]{1,0:T(8,128)(2,1)S(1)} %reshape.221, bf16[1,4096,2048]{2,1,0:T(8,128)(2,1)} %param.27), kind=kOutput, calls=%fused_computation.4 | convolution fusion | flops 805306368 | bytes 17563648 | tf_op jit(solution)/shard_map/dot_general | solution.py:94
  77.4 0.0 copy-start.1
  77.4 0.0 copy-start.3
  77.4 0.0 copy-start.2
  77.4 0.0 copy-start.4
  77.5 13.7 %fusion.7 = bf16[48,4096]{1,0:T(8,128)(2,1)S(1)} fusion(bf16[1,2048,4096]{2,1,0:T(8,128)(2,1)} %param.29, bf16[48,4096]{1,0:T(8,128)(2,1)S(1)} %reshape.221, bf16[1,4096,2048]{2,1,0:T(8,128)(2,1)} %param.28, f32[48,2048]{1,0:T(8,128)S(1)} %fusion.5), kind=kOutput, calls=%fused_computation.6 | convolution fusion | flops 1611399168 | bytes 34734080 | tf_op jit(solution)/shard_map/dot_general | solution.py:99
  91.1 16.0 %fusion = bf16[16,4096]{1,0:T(8,128)(2,1)S(1)} fusion(bf16[48,4096]{1,0:T(8,128)(2,1)S(1)} %fusion.7), kind=kCustom, calls=%all-reduce-scatter | all-reduce-scatter fusion | flops 262145 | bytes 524800
  107.2 2.8 %collective-permute-start = (bf16[12,4096]{1,0:T(8,128)(2,1)S(1)}, bf16[12,4096]{1,0:T(8,128)(2,1)S(1)}, u32[]{:S(2)}, u32[]{:S(2)}) collective-permute-start(bf16[12,4096]{1,0:T(8,128)(2,1)S(1)} %slice.8), channel_id=1, source_target_pairs={{0,4},{4,8},{8,12},{1,5},{5,9},{9,13},{2,6},{6,10},{10,14},{3,7},{... | collective-permute-start | bytes 294920
  110.0 0.0 copy-done.1
  110.1 0.0 copy-done.3
  110.1 0.2 fusion.43
  110.3 0.0 copy-done.2
  110.4 0.1 multiply_reduce_fusion
  110.5 0.1 convolution_bitcast_fusion
  110.6 2.0 %collective-permute-done = bf16[12,4096]{1,0:T(8,128)(2,1)S(1)} collective-permute-done((bf16[12,4096]{1,0:T(8,128)(2,1)S(1)}, bf16[12,4096]{1,0:T(8,128)(2,1)S(1)}, u32[]{:S(2)}, u32[]{:S(2)}) %collective-permute-start) | collective-permute-done | bytes 98336
  112.5 0.3 concatenate
  112.9 1.0 fusion.10
  113.9 0.0 all-reduce.8.cloned.1.call-update
  113.9 0.0 copy-done.4
  113.9 0.6 dynamic-slice.2
  115.1 31.0 %all-reduce.8.cloned.1.call-done = bf16[16,4096]{1,0:T(8,128)(2,1)} async-done(((bf16[16,4096]{1,0:T(8,128)(2,1)}), bf16[16,4096]{1,0:T(8,128)(2,1)}) %all-reduce.8.cloned.1.call-update) | async-done | bytes 131088
  146.1 1.5 constant_dynamic-slice_fusion
  (12 shorter events, 0.2 us)
Async XLA Ops:
  6.5 2.3 %copy-start = (bf16[16,1,256,128]{3,2,1,0:T(8,128)(2,1)S(1)}, bf16[16,1,256,128]{3,2,1,0:T(8,128)(2,1)}, u32[]{:S(2)}) copy-start(bf16[16,1,256,128]{3,2,1,0:T(8,128)(2,1)} %param.19) | copy-start | bytes 3145732
  6.5 44.7 %all-reduce.6.cloned.1.call-start = ((), (), s32[]{:S(2)}) async-start(), calls=%async_computation | async-start | bytes 524288 | tf_op jit(solution)/shard_map/psum | solution.py:78
  16.1 130.0 %all-reduce.8.cloned.1.call-start = ((), (), s32[]{:S(2)}) async-start(), calls=%async_computation.1 | async-start | bytes 262144
  77.4 32.6 %copy-start.1 = (f32[4096]{0:T(1024)S(1)}, f32[4096]{0:T(1024)}, u32[]{:S(2)}) copy-start(f32[4096]{0:T(1024)} %param.24) | copy-start | bytes 49156
  77.4 32.6 %copy-start.3 = (bf16[4096,4]{0,1:T(4,128)(2,1)S(1)}, bf16[4096,4]{0,1:T(4,128)(2,1)}, u32[]{:S(2)}) copy-start(bf16[4096,4]{0,1:T(4,128)(2,1)} %param.25) | copy-start | bytes 98308
  77.4 32.9 %copy-start.2 = (s32[16,2]{0,1:T(2,128)S(1)}, s32[16,2]{0,1:T(2,128)}, u32[]{:S(2)}) copy-start(s32[16,2]{0,1:T(2,128)} %param.26) | copy-start | bytes 388
  77.4 36.4 %copy-start.4 = (u32[32]{0:T(128)S(1)}, u32[32]{0:T(128)}, u32[]{:S(2)}) copy-start(u32[32]{0:T(128)} %constant.45) | copy-start | bytes 388
  107.2 5.4 %collective-permute-start = (bf16[12,4096]{1,0:T(8,128)(2,1)S(1)}, bf16[12,4096]{1,0:T(8,128)(2,1)S(1)}, u32[]{:S(2)}, u32[]{:S(2)}) collective-permute-start(bf16[12,4096]{1,0:T(8,128)(2,1)S(1)} %slice.8), channel_id=1, source_target_pairs={{0,4},{4,8},{8,12},{1,5},{5,9},{9,13},{2,6},{6,10},{10,14},{3,7},{... | collective-permute-start | bytes 294920
Sparse Core Ops, SparseCore 0:
  16.2 34.9 all-reduce.5
  114.0 32.0 all-reduce.7
where the time goes:
time: 155 us; the launch traced here: 154 us
  waiting for transfers between devices  65.2 us (42%)
  matrix products  31.9 us (21%)
  blocking collectives  31.2 us (20%)
  between operations  14.9 us (10%)
  other arithmetic  4.53 us (3%)
  local copies, waits for them, and re-layouts  3.85 us (2%)
  starting transfers between devices  2.89 us (2%)
    unnamed x4, waiting for transfers between devices  33 us
    psum x1, waiting for transfers between devices, body(): summed = lax.psum(partial_value, 'expert')  32.2 us
    unnamed x1, blocking collectives  16 us
    all_gather x1, blocking collectives, body(): block_rows = lax.all_gather(sent_rows, 'batch', axis=0, tiled=True)  15.2 us
    dot_general x1, matrix products, body(): jnp.dot(block_rows, w_down[0], preferred_element_type=jnp.float32)  13.7 us
    dot_general x1, matrix products, body(): jnp.dot(block_rows, w_gate[0], preferred_element_type=jnp.float32)  8.79 us
    unnamed x16, local copies, waits for them, and re-layouts  3.76 us
    dot_general x1, matrix products, body(): jnp.dot(attended, out_weight, preferred_element_type=jnp.float32)  3.56 us
  transfers between devices with their start and end apart: 3, of which 3 were waited for; matrix products, arithmetic and copies ran while one was open for 2% of the time, Pallas kernels for 0%

commit v1 on v0

--- a/solution.py
+++ b/solution.py
@@ -75,7 +75,8 @@
     my_expert = lax.axis_index("expert")
     attended = attend(queries, key_new, value_new, key_cache, value_cache, cache_len, new_slot)
     partial_value = jnp.dot(attended, out_weight, preferred_element_type=jnp.float32)
-    summed = lax.psum(partial_value, "expert")
+    guide_samples = lambda obj, ax_name: jnp.sum(lax.all_gather(obj, ax_name), axis=0)
+    summed = guide_samples(partial_value, "expert")
     stream = (residual_in.astype(jnp.float32) + summed).astype(jnp.bfloat16)
     values = stream.astype(jnp.float32)
     scaling = lax.rsqrt(jnp.mean(values * values, axis=1, keepdims=True) + epsilon)

time: 155 us -> 141 us (0.910)
  waiting for transfers between devices: 65.2 us -> 48.8 us
  blocking collectives: 31.2 us -> 33.8 us
  starting transfers between devices: 2.89 us -> 1.34 us
    psum x1 -> x0, waiting for transfers between devices: 32.2 us -> none  [body(): summed = lax.psum(partial_value, 'expert')]
    all_gather x0 -> x1, waiting for transfers between devices: none -> 16.6 us  [body(): lax.all_gather(obj, ax_name)]
    unnamed x1, blocking collectives: 16 us -> 17.8 us
    unnamed x2, starting transfers between devices: 2.89 us -> 1.34 us
where the time goes in v1:
time: 141 us; the launch traced here: 140 us
  waiting for transfers between devices  48.8 us (35%)
  blocking collectives  33.8 us (24%)
  matrix products  31.9 us (23%)
  between operations  14.9 us (11%)
  other arithmetic  5.76 us (4%)
  local copies, waits for them, and re-layouts  3.85 us (3%)
    unnamed x4, waiting for transfers between devices  32.2 us
    unnamed x1, blocking collectives  17.8 us
    all_gather x1, waiting for transfers between devices, body(): lax.all_gather(obj, ax_name)  16.6 us
    all_gather x1, blocking collectives, body(): block_rows = lax.all_gather(sent_rows, 'batch', axis=0, tiled=True)  16 us
    dot_general x1, matrix products, body(): jnp.dot(block_rows, w_down[0], preferred_element_type=jnp.float32)  13.7 us
    dot_general x1, matrix products, body(): jnp.dot(block_rows, w_gate[0], preferred_element_type=jnp.float32)  8.79 us
    unnamed x16, local copies, waits for them, and re-layouts  3.76 us
    dot_general x1, matrix products, body(): jnp.dot(attended, out_weight, preferred_element_type=jnp.float32)  3.58 us
  transfers between devices with their start and end apart: 3, of which 3 were waited for; matrix products, arithmetic and copies ran while one was open for 2% of the time, Pallas kernels for 0%

profile of v1, /device:TPU:0, one launch (start us, length us, event | category | flops | bytes accessed | tf_op | source)
XLA Modules:
  0.0 140.4 jit_solution(12201496424224028612)
XLA Ops:
  6.5 0.0 copy-start
  6.5 0.0 all-gather.4.cloned.1.call-start
  6.5 0.7 broadcast_compare_fusion
  7.3 0.7 fusion.48
  8.0 0.9 fusion.52
  8.9 0.0 copy-done
  8.9 1.2 fusion.67
  10.1 0.2 fusion.37
  10.3 0.7 bitcast_convert_fusion
  11.0 1.5 %fusion.19 = bf16[16,4,128]{2,1,0:T(4,128)(2,1)S(1)} fusion(bf16[16,1,256,128]{3,2,1,0:T(8,128)(2,1)} %param.20, f32[16,4,256]{2,1,0:T(4,128)S(1)} %get-tuple-element.12, f32[16,4]{1,0:T(8,128)S(1)} %get-tuple-element.10, f32[16,4]{1,0:T(8,128)S(1)} %multiply_maximum_fusion, pred[16,256]{1,0:T(8,128)(4,1)S(1)} %fusion.48, ...), kind=kOutput, calls=%fused_computation.16 | convolution fusion | flops 4284416 | bytes 1143552 | tf_op jit(solution)/shard_map/skgt,sktd->skgd/dot_general | solution.py:32
  12.5 3.6 %fusion.45 = f32[16,4096]{1,0:T(8,128)} fusion(bf16[512,4096]{1,0:T(8,128)(2,1)} %param.23, bf16[2,8,4,128]{3,2,1,0:T(4,128)(2,1)S(1)} %bitcast.58), kind=kOutput, calls=%fused_computation.45 | convolution fusion | flops 67108864 | bytes 4472832 | tf_op jit(solution)/shard_map/dot_general | solution.py:77
  16.1 0.0 all-gather.4.cloned.1.call-update
  16.1 0.0 all-reduce.5.cloned.1.call-start
  16.2 0.7 fusion.63
  16.9 0.1 copy.26
  17.0 0.1 reduce.6
  17.1 1.2 dynamic-slice.6
  19.0 16.6 %all-gather.4.cloned.1.call-done = f32[64,4096]{1,0:T(8,128)} async-done(((f32[16,4096]{1,0:T(8,128)}), f32[64,4096]{1,0:T(8,128)}) %all-gather.4.cloned.1.call-update) | async-done | bytes 1048592 | tf_op jit(solution)/shard_map/all_gather | solution.py:78
  35.7 1.3 reduce_sum.65
  37.0 1.1 fusion.29
  38.1 1.0 fusion.11
  39.0 16.0 %all-gather.1 = bf16[4,12,4096]{2,1,0:T(8,128)(2,1)S(1)} all-gather(bf16[1,12,4096]{2,1,0:T(8,128)(2,1)S(1)} %fusion.11), channel_id=1, replica_groups=mesh['group'=2,'batch'=4,'expert'=4] {'batch'}, dimensions={0}, use_global_device_ids=true | all-gather | bytes 491520 | tf_op jit(solution)/shard_map/all_gather | solution.py:94
  55.0 0.1 reshape.222
  55.1 8.8 %fusion.5 = f32[48,2048]{1,0:T(8,128)S(1)} fusion(bf16[48,4096]{1,0:T(8,128)(2,1)S(1)} %reshape.222, bf16[1,4096,2048]{2,1,0:T(8,128)(2,1)} %param.27), kind=kOutput, calls=%fused_computation.4 | convolution fusion | flops 805306368 | bytes 17563648 | tf_op jit(solution)/shard_map/dot_general | solution.py:95
  63.9 0.0 copy-start.1
  63.9 0.0 copy-start.3
  63.9 0.0 copy-start.2
  63.9 0.0 copy-start.4
  64.0 13.7 %fusion.7 = bf16[48,4096]{1,0:T(8,128)(2,1)S(1)} fusion(bf16[1,2048,4096]{2,1,0:T(8,128)(2,1)} %param.29, bf16[48,4096]{1,0:T(8,128)(2,1)S(1)} %reshape.222, bf16[1,4096,2048]{2,1,0:T(8,128)(2,1)} %param.28, f32[48,2048]{1,0:T(8,128)S(1)} %fusion.5), kind=kOutput, calls=%fused_computation.6 | convolution fusion | flops 1611399168 | bytes 34734080 | tf_op jit(solution)/shard_map/dot_general | solution.py:100
  77.6 17.8 %fusion = bf16[16,4096]{1,0:T(8,128)(2,1)S(1)} fusion(bf16[48,4096]{1,0:T(8,128)(2,1)S(1)} %fusion.7), kind=kCustom, calls=%all-reduce-scatter | all-reduce-scatter fusion | flops 262145 | bytes 524800
  95.5 1.3 collective-permute-start
  96.8 0.0 copy-done.1
  96.8 0.0 copy-done.3
  96.8 0.2 fusion.43
  97.1 0.0 copy-done.2
  97.1 0.1 multiply_reduce_fusion
  97.2 0.1 convolution_bitcast_fusion
  97.4 2.0 %collective-permute-done = bf16[12,4096]{1,0:T(8,128)(2,1)S(1)} collective-permute-done((bf16[12,4096]{1,0:T(8,128)(2,1)S(1)}, bf16[12,4096]{1,0:T(8,128)(2,1)S(1)}, u32[]{:S(2)}, u32[]{:S(2)}) %collective-permute-start) | collective-permute-done | bytes 98336
  99.3 0.3 concatenate
  99.6 1.0 fusion.10
  100.6 0.0 all-reduce.5.cloned.1.call-update
  100.7 0.0 copy-done.4
  100.7 0.6 dynamic-slice.2
  101.9 30.2 %all-reduce.5.cloned.1.call-done = bf16[16,4096]{1,0:T(8,128)(2,1)} async-done(((bf16[16,4096]{1,0:T(8,128)(2,1)}), bf16[16,4096]{1,0:T(8,128)(2,1)}) %all-reduce.5.cloned.1.call-update) | async-done | bytes 131088
  132.1 1.5 %constant_dynamic-slice_fusion = bf16[4,4096]{1,0:T(4,128)(2,1)} fusion(bf16[16,4096]{1,0:T(8,128)(2,1)} %all-reduce.5.cloned.1.call-done, u32[]{:T(128)S(6)} %multiply.9), kind=kLoop, calls=%fused_computation.76 | loop fusion | bytes 65540
  (12 shorter events, 0.2 us)
Async XLA Ops:
  6.5 2.3 %copy-start = (bf16[16,1,256,128]{3,2,1,0:T(8,128)(2,1)S(1)}, bf16[16,1,256,128]{3,2,1,0:T(8,128)(2,1)}, u32[]{:S(2)}) copy-start(bf16[16,1,256,128]{3,2,1,0:T(8,128)(2,1)} %param.19) | copy-start | bytes 3145732
  6.5 29.1 %all-gather.4.cloned.1.call-start = ((), (), s32[]{:S(2)}) async-start(), calls=%async_computation | async-start | bytes 1310720 | tf_op jit(solution)/shard_map/all_gather | solution.py:78
  16.1 116.0 %all-reduce.5.cloned.1.call-start = ((), (), s32[]{:S(2)}) async-start(), calls=%async_computation.1 | async-start | bytes 262144
  63.9 32.9 %copy-start.1 = (f32[4096]{0:T(1024)S(1)}, f32[4096]{0:T(1024)}, u32[]{:S(2)}) copy-start(f32[4096]{0:T(1024)} %param.24) | copy-start | bytes 49156
  63.9 32.9 %copy-start.3 = (bf16[4096,4]{0,1:T(4,128)(2,1)S(1)}, bf16[4096,4]{0,1:T(4,128)(2,1)}, u32[]{:S(2)}) copy-start(bf16[4096,4]{0,1:T(4,128)(2,1)} %param.25) | copy-start | bytes 98308
  63.9 33.1 %copy-start.2 = (s32[16,2]{0,1:T(2,128)S(1)}, s32[16,2]{0,1:T(2,128)}, u32[]{:S(2)}) copy-start(s32[16,2]{0,1:T(2,128)} %param.26) | copy-start | bytes 388
  63.9 36.7 %copy-start.4 = (u32[32]{0:T(128)S(1)}, u32[32]{0:T(128)}, u32[]{:S(2)}) copy-start(u32[32]{0:T(128)} %constant.45) | copy-start | bytes 388
  95.5 3.8 %collective-permute-start = (bf16[12,4096]{1,0:T(8,128)(2,1)S(1)}, bf16[12,4096]{1,0:T(8,128)(2,1)S(1)}, u32[]{:S(2)}, u32[]{:S(2)}) collective-permute-start(bf16[12,4096]{1,0:T(8,128)(2,1)S(1)} %slice.8), channel_id=1, source_target_pairs={{0,4},{4,8},{8,12},{1,5},{5,9},{9,13},{2,6},{6,10},{10,14},{3,7},{... | collective-permute-start | bytes 294920
Sparse Core Ops, SparseCore 0:
  16.2 19.4 all-gather.3
  100.8 31.2 all-reduce.4
